TPU v7x, 32 devices: a whole 2x2x4 slice. The times are simulated.
32 devices in a mesh: wide: 8 (over z, core), narrow: 4 (over y, x).
Axes of the slice: x: 2, y: 2, z: 4, core: 2. Of those that a mesh axis runs over, the one named last changes fastest.
Arguments:
- tridiag_vectors: float32 [128, 131072], P(('wide', 'narrow')), may hold values from -6 to 6
- reflectors: float32 [2, 131072, 256], P(None, 'wide'), may hold values from -0.015625 to 0.015625
- triangles: float32 [2, 256, 256], replicated, as said below
- lower_blocks: float32 [6, 1536, 1536], P(None, 'wide'), may hold values from -0.109375 to 0.109375
- diag_inverses: float32 [4, 1536, 1536], P(None, None, 'wide'), as said below
Outputs:
- transformed: float32 [128, 131072], P('narrow', 'wide')
- solved: float32 [128, 4, 1536], P('narrow', None, 'wide')
Inputs may be any that keep to these rules, and one draw needn't show every extreme that they name: `triangles`: zero below the diagonal, positive on it. `diag_inverses`: zero above the diagonal, positive on it.
All inputs are finite; a program needn't handle non-finite values.
Results may differ from a plain program's by a relative error of at most 0.00019.
Values sent between devices are 32-bit elements; how exact they have to be, the bound alone decides.
A program may use at most 128 MiB of HBM per device.

v0:
```python
import jax
import jax.numpy as jnp
from jax import lax
from jax.sharding import PartitionSpec as P

HIGHEST = lax.Precision.HIGHEST


def reflect(current, vectors, factor, products):
    coeffs = jnp.dot(products, factor.T, precision=HIGHEST)
    return current - jnp.dot(coeffs, vectors.T, precision=HIGHEST)


def add_piece(inverse, segment):
    return jnp.dot(segment, inverse, precision=HIGHEST)


def solve_chain(corner, lower_blocks, diag_inverses):
    local_count, panels, share_cols = corner.shape
    zeroed = jnp.zeros((local_count, share_cols), jnp.float32)
    pending = [zeroed] * panels
    results = [zeroed] * panels
    for source in reversed(range(panels)):
        remain = corner[:, source, :] - pending[source]
        solution = add_piece(
            diag_inverses[source], lax.all_gather(remain, "wide", axis=1, tiled=True)
        )
        results[source] = solution
        if source > 0:
            offset = source * (source - 1) // 2
            blocks = lower_blocks[offset : offset + source]
            partial_terms = jnp.einsum("ks,qsc->kqc", solution, blocks, precision=HIGHEST)
            scattered = lax.psum_scatter(partial_terms, "wide", scatter_dimension=2, tiled=True)
            for target in range(source):
                pending[target] = pending[target] + scattered[:, target, :]
    return jnp.stack(results, axis=1)


def body(tridiag_vectors, reflectors, triangles, lower_blocks, diag_inverses):
    wide_size = lax.axis_size("wide")
    spread = lax.all_to_all(
        tridiag_vectors, ("wide", "narrow"), split_axis=1, concat_axis=0, tiled=True
    )
    current = lax.all_to_all(spread, "narrow", split_axis=0, concat_axis=1, tiled=True)
    for which in (1, 0):
        products = lax.psum(jnp.dot(current, reflectors[which], precision=HIGHEST), "wide")
        current = reflect(current, reflectors[which], triangles[which], products)
    panels, panel_rows, share_cols = diag_inverses.shape
    corner_span = panels * panel_rows
    tail_cols = current[:, current.shape[1] - corner_span :]
    framed = tail_cols.reshape(tail_cols.shape[0], panels, wide_size, share_cols)
    received = lax.all_to_all(framed, "wide", split_axis=2, concat_axis=2, tiled=True)
    corner = received[:, :, wide_size - 1, :]
    solved = solve_chain(corner, lower_blocks, diag_inverses)
    return (current, solved)


def solution(mesh):
    placed = (
        P(("wide", "narrow"), None),
        P(None, "wide", None),
        P(),
        P(None, "wide", None),
        P(None, None, "wide"),
    )
    return jax.shard_map(
        body,
        mesh=mesh,
        in_specs=placed,
        out_specs=(P("narrow", "wide"), P("narrow", None, "wide")),
        check_vma=False,
    )
```

profile of v0, /device:TPU:0, one launch (start us, length us, event | category | flops | bytes accessed | tf_op | source)
XLA Modules:
  0.0 433.0 jit_solution(8765695923981802089)
XLA Ops:
  7.2 56.5 %all_to_all.40 = f32[4,32,4096]{2,0,1:T(4,128)} all-to-all(f32[4,32,4096]{2,0,1:T(4,128)} %bitcast.93), channel_id=1, replica_groups=mesh['wide'=8,'narrow'=4] {'wide','narrow'}, dimensions={1} | all-to-all | bytes 4194304 | tf_op jit(solution)/shard_map/all_to_all | solution.py:41
  65.6 28.2 %all_to_all.41 = f32[4,32,4096]{2,1,0:T(8,128)S(1)} all-to-all(f32[4,32,4096]{2,1,0:T(8,128)S(1)} %all_to_all.32), channel_id=1, replica_groups=mesh['wide'=8,'narrow'=4] {'narrow'}, dimensions={0} | all-to-all | bytes 4194304 | tf_op jit(solution)/shard_map/all_to_all | solution.py:44
  95.3 10.7 %fusion.4 = f32[32,256]{1,0:T(8,128)S(1)} fusion(f32[32,16384]{1,0:T(8,128)S(1)} %bitcast.83, f32[2,16384,256]{2,1,0:T(8,128)} %param.6), kind=kOutput, calls=%fused_computation.6 | convolution fusion | flops 1610612736 | bytes 18907136 | tf_op jit(solution)/shard_map/dot_general | solution.py:46
  106.0 26.1 %psum.14 = f32[32,256]{1,0:T(8,128)S(1)} all-reduce(f32[32,256]{1,0:T(8,128)S(1)} %fusion.4), channel_id=1, replica_groups=mesh['wide'=8,'narrow'=4] {'wide'}, use_global_device_ids=true, to_apply=%region_0.0 | all-reduce | flops 8192 | bytes 65536 | tf_op jit(solution)/shard_map/psum | solution.py:46
  132.5 18.6 %convolution_subtract_fusion.1 = f32[32,16384]{1,0:T(8,128)S(1)} fusion(f32[32,16384]{1,0:T(8,128)} %bitcast.84, f32[32,256]{1,0:T(8,128)S(1)} %fusion.33, f32[2,16384,256]{2,1,0:T(8,128)} %param.6), kind=kOutput, calls=%fused_computation.1 | convolution fusion | flops 1611137024 | bytes 21004288 | tf_op jit(solution)/shard_map/dot_general | solution.py:11
  151.1 10.6 %fusion.1 = f32[32,256]{1,0:T(8,128)S(1)} fusion(f32[32,16384]{1,0:T(8,128)S(1)} %convolution_subtract_fusion.1, f32[2,16384,256]{2,1,0:T(8,128)} %param.6), kind=kOutput, calls=%fused_computation.3 | convolution fusion | flops 1610612736 | bytes 18907136 | tf_op jit(solution)/shard_map/dot_general | solution.py:46
  161.8 26.2 %psum.15 = f32[32,256]{1,0:T(8,128)S(1)} all-reduce(f32[32,256]{1,0:T(8,128)S(1)} %fusion.1), channel_id=1, replica_groups=mesh['wide'=8,'narrow'=4] {'wide'}, use_global_device_ids=true, to_apply=%region_1.0 | all-reduce | flops 8192 | bytes 65536 | tf_op jit(solution)/shard_map/psum | solution.py:46
  188.3 17.3 %convolution_subtract_fusion = f32[32,16384]{1,0:T(8,128)S(1)} fusion(f32[32,16384]{1,0:T(8,128)S(1)} %convolution_subtract_fusion.1, f32[32,256]{1,0:T(8,128)S(1)} %fusion.31, f32[2,16384,256]{2,1,0:T(8,128)} %param.6), kind=kOutput, calls=%fused_computation | convolution fusion | flops 1611137024 | bytes 21004288 | tf_op jit(solution)/shard_map/dot_general | solution.py:11
  208.0 29.0 %all_to_all.42 = f32[32,4,8,192]{3,0,1,2:T(8,128)S(1)} all-to-all(f32[32,4,8,192]{3,0,1,2:T(8,128)S(1)} %copy.22), channel_id=1, replica_groups=mesh['wide'=8,'narrow'=4] {'wide'}, dimensions={2} | all-to-all | bytes 1572864 | tf_op jit(solution)/shard_map/all_to_all | solution.py:52
  237.1 15.7 %all-gather = f32[32,1,1536]{0,1,2:T(1,128)S(1)} all-gather(f32[32,1,192]{0,1,2:T(1,128)S(1)} %copy.23), channel_id=2, replica_groups=mesh['wide'=8,'narrow'=4] {'wide'}, dimensions={2}, use_global_device_ids=true | all-gather | bytes 221184 | tf_op jit(solution)/shard_map/all_gather | solution.py:26
  252.9 2.6 fusion.21
  255.5 5.0 %fusion.10 = f32[32,3,1536]{2,0,1:T(8,128)} fusion(f32[6,192,1536]{2,1,0:T(8,128)} %param.8, f32[32,192]{1,0:T(8,128)S(1)} %fusion.21), kind=kOutput, calls=%fused_computation.12 | convolution fusion | flops 339738624 | bytes 4153344 | tf_op jit(solution)/shard_map/ks,qsc->kqc/dot_general | solution.py:32
  260.5 2.6 copy.28
  265.5 29.5 %reduce-scatter.10.cloned.1.call-done = f32[192,96]{1,0:T(8,128)} async-done(((f32[1536,96]{1,0:T(8,128)}), f32[192,96]{1,0:T(8,128)}) %reduce-scatter.10.cloned.1.call-update) | async-done | bytes 73744
  296.5 16.0 %all-gather.1 = f32[32,1,1536]{0,1,2:T(1,128)S(1)} all-gather(f32[32,1,192]{0,1,2:T(1,128)S(1)} %copy.24), channel_id=3, replica_groups=mesh['wide'=8,'narrow'=4] {'wide'}, dimensions={2}, use_global_device_ids=true | all-gather | bytes 221184 | tf_op jit(solution)/shard_map/all_gather | solution.py:26
  312.5 2.6 fusion.19
  315.1 3.2 fusion.12
  321.0 30.2 %reduce-scatter.12.cloned.1.call-done = f32[192,64]{1,0:T(8,128)} async-done(((f32[1536,64]{1,0:T(8,128)}), f32[192,64]{1,0:T(8,128)}) %reduce-scatter.12.cloned.1.call-update) | async-done | bytes 49168
  352.6 15.7 %all-gather.2 = f32[32,1,1536]{0,1,2:T(1,128)S(1)} all-gather(f32[32,1,192]{0,1,2:T(1,128)S(1)} %copy.25), channel_id=4, replica_groups=mesh['wide'=8,'narrow'=4] {'wide'}, dimensions={2}, use_global_device_ids=true | all-gather | bytes 221184 | tf_op jit(solution)/shard_map/all_gather | solution.py:26
  368.4 2.6 fusion.17
  371.0 4.8 %convolution_bitcast_fusion = f32[1536,32]{1,0:T(8,128)} fusion(f32[32,192]{1,0:T(8,128)S(1)} %fusion.17, f32[6,192,1536]{2,1,0:T(8,128)} %param.8), kind=kOutput, calls=%fused_computation.14 | convolution fusion | flops 113246208 | bytes 1400832 | tf_op jit(solution)/shard_map/ks,qsc->kqc/dot_general | solution.py:32
  375.9 30.3 %reduce-scatter.14.cloned.1.call-done = f32[192,32]{1,0:T(8,128)} async-done(((f32[1536,32]{1,0:T(8,128)}), f32[192,32]{1,0:T(8,128)}) %reduce-scatter.14.cloned.1.call-update) | async-done | bytes 24592
  407.3 15.7 %all-gather.3 = f32[32,1,1536]{0,1,2:T(1,128)S(1)} all-gather(f32[32,1,192]{0,1,2:T(1,128)S(1)} %copy.26), channel_id=5, replica_groups=mesh['wide'=8,'narrow'=4] {'wide'}, dimensions={2}, use_global_device_ids=true | all-gather | bytes 221184 | tf_op jit(solution)/shard_map/all_gather | solution.py:26
  423.1 2.6 fusion.28
  (43 shorter events, 16.5 us)
Async XLA Ops:
  7.2 287.9 %reduce-scatter.10.cloned.1.call-start = ((), (), s32[]{:S(2)}) async-start(), calls=%async_computation.6 | async-start | bytes 884736
  94.0 1.3 copy-start
  95.3 36.8 %copy-start.2 = (f32[2,256,256]{2,1,0:T(8,128)S(1)}, f32[2,256,256]{2,1,0:T(8,128)}, u32[]{:S(2)}) copy-start(f32[2,256,256]{2,1,0:T(8,128)} %param.7) | copy-start | bytes 1572868
  205.5 1.3 copy-start.1
  265.4 85.8 %reduce-scatter.12.cloned.1.call-start = ((), (), s32[]{:S(2)}) async-start(), calls=%async_computation.7 | async-start | bytes 884736
  320.9 85.4 %reduce-scatter.14.cloned.1.call-start = ((), (), s32[]{:S(2)}) async-start(), calls=%async_computation.8 | async-start | bytes 884736
Sparse Core Ops, SparseCore 0:
  265.6 29.4 reduce-scatter.9
  321.0 30.1 reduce-scatter.11
  375.9 30.2 reduce-scatter.13
where the time goes:
time: 434 us; the launch traced here: 433 us
  blocking collectives  229 us (53%)
  waiting for transfers between devices  90.1 us (21%)
  matrix products  81.5 us (19%)
  local copies, waits for them, and re-layouts  18.2 us (4%)
  between operations  14 us (3%)
    unnamed x6, waiting for transfers between devices  90.1 us
    all_gather x4, blocking collectives, solve_chain(): lax.all_gather(remain, 'wide', axis=1, tiled=True)  63.2 us
    all_to_all x1, blocking collectives, body(): lax.all_to_all(tridiag_vectors, ('wide', 'narrow'), split_axis=1, concat_...  56.5 us
    psum x2, blocking collectives, body(): lax.psum(jnp.dot(current, reflectors[which], precision=HIGHEST), 'wide')  52.3 us
    dot_general x2, matrix products, reflect(): return current - jnp.dot(coeffs, vectors.T, precision=HIGHEST)  35.9 us
    all_to_all x1, blocking collectives, body(): lax.all_to_all(framed, 'wide', split_axis=2, concat_axis=2, tiled=True)  29 us
    all_to_all x1, blocking collectives, body(): lax.all_to_all(spread, 'narrow', split_axis=0, concat_axis=1, tiled=True)  28.2 us
    dot_general x2, matrix products, body(): jnp.dot(current, reflectors[which], precision=HIGHEST)  21.3 us
  transfers between devices with their start and end apart: 3, of which 3 were waited for; matrix products, arithmetic and copies ran while one was open for 0% of the time, Pallas kernels for 0%

commit v1 on v0

--- a/solution.py
+++ b/solution.py
@@ -38,8 +38,14 @@
 
 def body(tridiag_vectors, reflectors, triangles, lower_blocks, diag_inverses):
     wide_size = lax.axis_size("wide")
-    spread = lax.all_to_all(
-        tridiag_vectors, ("wide", "narrow"), split_axis=1, concat_axis=0, tiled=True
+    spread = jnp.concatenate(
+        lax.all_to_all(
+            jnp.stack(jnp.split(tridiag_vectors, lax.axis_size(("wide", "narrow")), axis=1)),
+            ("wide", "narrow"),
+            0,
+            0,
+        ),
+        axis=0,
     )
     current = lax.all_to_all(spread, "narrow", split_axis=0, concat_axis=1, tiled=True)
     for which in (1, 0):

time: 434 us -> 463 us (1.067)
  local copies, waits for them, and re-layouts: 18.2 us -> 45.2 us
    unnamed x19 -> x50, local copies, waits for them, and re-layouts: 14.2 us -> 40.6 us
where the time goes in v1:
time: 463 us; the launch traced here: 461 us
  blocking collectives  230 us (50%)
  waiting for transfers between devices  90 us (19%)
  matrix products  81.5 us (18%)
  local copies, waits for them, and re-layouts  45.2 us (10%)
  between operations  14 us (3%)
    unnamed x6, waiting for transfers between devices  90 us
    all_gather x4, blocking collectives, solve_chain(): lax.all_gather(remain, 'wide', axis=1, tiled=True)  63.2 us
    all_to_all x1, blocking collectives, body(): lax.all_to_all(jnp.stack(jnp.split(tridiag_vectors, lax.axis_size(('wide'...  56.1 us
    psum x2, blocking collectives, body(): lax.psum(jnp.dot(current, reflectors[which], precision=HIGHEST), 'wide')  52.3 us
    unnamed x50, local copies, waits for them, and re-layouts  40.6 us
    dot_general x2, matrix products, reflect(): return current - jnp.dot(coeffs, vectors.T, precision=HIGHEST)  35.9 us
    all_to_all x1, blocking collectives, body(): lax.all_to_all(spread, 'narrow', split_axis=0, concat_axis=1, tiled=True)  29.1 us
    all_to_all x1, blocking collectives, body(): lax.all_to_all(framed, 'wide', split_axis=2, concat_axis=2, tiled=True)  29 us
  transfers between devices with their start and end apart: 3, of which 3 were waited for; matrix products, arithmetic and copies ran while one was open for 0% of the time, Pallas kernels for 0%

profile of v1, /device:TPU:0, one launch (start us, length us, event | category | flops | bytes accessed | tf_op | source)
XLA Modules:
  0.0 460.5 jit_solution(985742255214312461)
XLA Ops:
  34.5 56.1 %all_to_all.29 = f32[32,4,4096]{2,1,0:T(4,128)S(1)} all-to-all(f32[32,4,4096]{2,1,0:T(4,128)S(1)} %constant_dynamic-update-slice_fusion), channel_id=1, replica_groups=mesh['wide'=8,'narrow'=4] {'wide','narrow'}, dimensions={0} | all-to-all | bytes 4194304 | tf_op jit(solution)/shard_map/all_to_all | solution.py:42
  92.4 29.1 %all_to_all.30 = f32[4,32,4096]{2,1,0:T(8,128)S(1)} all-to-all(f32[4,32,4096]{2,1,0:T(8,128)} %all_to_all.21), channel_id=1, replica_groups=mesh['wide'=8,'narrow'=4] {'narrow'}, dimensions={0} | all-to-all | bytes 4194304 | tf_op jit(solution)/shard_map/all_to_all | solution.py:50
  122.9 10.7 %fusion.4 = f32[32,256]{1,0:T(8,128)S(1)} fusion(f32[32,16384]{1,0:T(8,128)S(1)} %bitcast.145, f32[2,16384,256]{2,1,0:T(8,128)} %param.6), kind=kOutput, calls=%fused_computation.6 | convolution fusion | flops 1610612736 | bytes 18907136 | tf_op jit(solution)/shard_map/dot_general | solution.py:52
  133.6 26.2 %psum.14 = f32[32,256]{1,0:T(8,128)S(1)} all-reduce(f32[32,256]{1,0:T(8,128)S(1)} %fusion.4), channel_id=1, replica_groups=mesh['wide'=8,'narrow'=4] {'wide'}, use_global_device_ids=true, to_apply=%region_0.0 | all-reduce | flops 8192 | bytes 65536 | tf_op jit(solution)/shard_map/psum | solution.py:52
  160.1 18.6 %convolution_subtract_fusion.1 = f32[32,16384]{1,0:T(8,128)S(1)} fusion(f32[32,16384]{1,0:T(8,128)} %bitcast.146, f32[32,256]{1,0:T(8,128)S(1)} %fusion.33, f32[2,16384,256]{2,1,0:T(8,128)} %param.6), kind=kOutput, calls=%fused_computation.1 | convolution fusion | flops 1611137024 | bytes 21004288 | tf_op jit(solution)/shard_map/dot_general | solution.py:11
  178.8 10.6 %fusion.1 = f32[32,256]{1,0:T(8,128)S(1)} fusion(f32[32,16384]{1,0:T(8,128)S(1)} %convolution_subtract_fusion.1, f32[2,16384,256]{2,1,0:T(8,128)} %param.6), kind=kOutput, calls=%fused_computation.3 | convolution fusion | flops 1610612736 | bytes 18907136 | tf_op jit(solution)/shard_map/dot_general | solution.py:52
  189.4 26.2 %psum.15 = f32[32,256]{1,0:T(8,128)S(1)} all-reduce(f32[32,256]{1,0:T(8,128)S(1)} %fusion.1), channel_id=1, replica_groups=mesh['wide'=8,'narrow'=4] {'wide'}, use_global_device_ids=true, to_apply=%region_1.0 | all-reduce | flops 8192 | bytes 65536 | tf_op jit(solution)/shard_map/psum | solution.py:52
  215.9 17.3 %convolution_subtract_fusion = f32[32,16384]{1,0:T(8,128)S(1)} fusion(f32[32,16384]{1,0:T(8,128)S(1)} %convolution_subtract_fusion.1, f32[32,256]{1,0:T(8,128)S(1)} %fusion.31, f32[2,16384,256]{2,1,0:T(8,128)} %param.6), kind=kOutput, calls=%fused_computation | convolution fusion | flops 1611137024 | bytes 21004288 | tf_op jit(solution)/shard_map/dot_general | solution.py:11
  235.7 29.0 %all_to_all.31 = f32[32,4,8,192]{3,0,1,2:T(8,128)S(1)} all-to-all(f32[32,4,8,192]{3,0,1,2:T(8,128)S(1)} %copy.17), channel_id=1, replica_groups=mesh['wide'=8,'narrow'=4] {'wide'}, dimensions={2} | all-to-all | bytes 1572864 | tf_op jit(solution)/shard_map/all_to_all | solution.py:58
  264.8 15.7 %all-gather = f32[32,1,1536]{0,1,2:T(1,128)S(1)} all-gather(f32[32,1,192]{0,1,2:T(1,128)S(1)} %copy.18), channel_id=2, replica_groups=mesh['wide'=8,'narrow'=4] {'wide'}, dimensions={2}, use_global_device_ids=true | all-gather | bytes 221184 | tf_op jit(solution)/shard_map/all_gather | solution.py:26
  280.5 2.6 fusion.21
  283.2 5.0 %fusion.10 = f32[32,3,1536]{2,0,1:T(8,128)} fusion(f32[6,192,1536]{2,1,0:T(8,128)} %param.8, f32[32,192]{1,0:T(8,128)S(1)} %fusion.21), kind=kOutput, calls=%fused_computation.12 | convolution fusion | flops 339738624 | bytes 4153344 | tf_op jit(solution)/shard_map/ks,qsc->kqc/dot_general | solution.py:32
  288.2 2.6 copy.23
  293.2 29.4 %reduce-scatter.10.cloned.1.call-done = f32[192,96]{1,0:T(8,128)} async-done(((f32[1536,96]{1,0:T(8,128)}), f32[192,96]{1,0:T(8,128)}) %reduce-scatter.10.cloned.1.call-update) | async-done | bytes 73744
  324.1 16.0 %all-gather.1 = f32[32,1,1536]{0,1,2:T(1,128)S(1)} all-gather(f32[32,1,192]{0,1,2:T(1,128)S(1)} %copy.19), channel_id=3, replica_groups=mesh['wide'=8,'narrow'=4] {'wide'}, dimensions={2}, use_global_device_ids=true | all-gather | bytes 221184 | tf_op jit(solution)/shard_map/all_gather | solution.py:26
  340.1 2.6 fusion.19
  342.7 3.2 fusion.12
  348.6 30.2 %reduce-scatter.12.cloned.1.call-done = f32[192,64]{1,0:T(8,128)} async-done(((f32[1536,64]{1,0:T(8,128)}), f32[192,64]{1,0:T(8,128)}) %reduce-scatter.12.cloned.1.call-update) | async-done | bytes 49168
  380.2 15.7 %all-gather.2 = f32[32,1,1536]{0,1,2:T(1,128)S(1)} all-gather(f32[32,1,192]{0,1,2:T(1,128)S(1)} %copy.20), channel_id=4, replica_groups=mesh['wide'=8,'narrow'=4] {'wide'}, dimensions={2}, use_global_device_ids=true | all-gather | bytes 221184 | tf_op jit(solution)/shard_map/all_gather | solution.py:26
  395.9 2.6 fusion.17
  398.6 4.8 %convolution_bitcast_fusion = f32[1536,32]{1,0:T(8,128)} fusion(f32[32,192]{1,0:T(8,128)S(1)} %fusion.17, f32[6,192,1536]{2,1,0:T(8,128)} %param.8), kind=kOutput, calls=%fused_computation.14 | convolution fusion | flops 113246208 | bytes 1400832 | tf_op jit(solution)/shard_map/ks,qsc->kqc/dot_general | solution.py:32
  403.5 30.3 %reduce-scatter.14.cloned.1.call-done = f32[192,32]{1,0:T(8,128)} async-done(((f32[1536,32]{1,0:T(8,128)}), f32[192,32]{1,0:T(8,128)}) %reduce-scatter.14.cloned.1.call-update) | async-done | bytes 24592
  434.9 15.7 %all-gather.3 = f32[32,1,1536]{0,1,2:T(1,128)S(1)} all-gather(f32[32,1,192]{0,1,2:T(1,128)S(1)} %copy.21), channel_id=5, replica_groups=mesh['wide'=8,'narrow'=4] {'wide'}, dimensions={2}, use_global_device_ids=true | all-gather | bytes 221184 | tf_op jit(solution)/shard_map/all_gather | solution.py:26
  450.6 2.6 fusion.28
  (75 shorter events, 43.5 us)
Async XLA Ops:
  7.2 315.4 %reduce-scatter.10.cloned.1.call-start = ((), (), s32[]{:S(2)}) async-start(), calls=%async_computation.6 | async-start | bytes 884736
  121.6 1.3 copy-start
  122.9 36.9 %copy-start.2 = (f32[2,256,256]{2,1,0:T(8,128)S(1)}, f32[2,256,256]{2,1,0:T(8,128)}, u32[]{:S(2)}) copy-start(f32[2,256,256]{2,1,0:T(8,128)} %param.7) | copy-start | bytes 1572868
  233.2 1.3 copy-start.1
  293.1 85.7 %reduce-scatter.12.cloned.1.call-start = ((), (), s32[]{:S(2)}) async-start(), calls=%async_computation.7 | async-start | bytes 884736
  348.5 85.3 %reduce-scatter.14.cloned.1.call-start = ((), (), s32[]{:S(2)}) async-start(), calls=%async_computation.8 | async-start | bytes 884736
Sparse Core Ops, SparseCore 0:
  293.2 29.3 reduce-scatter.9
  348.6 30.1 reduce-scatter.11
  403.5 30.2 reduce-scatter.13
